TPU v7x, 32 devices: a whole 2x2x4 slice. The times are simulated.
32 devices in a mesh: elem: 16 (over z, y, core), test: 2 (over x).
Axes of the slice: x: 2, y: 2, z: 4, core: 2. Of those that a mesh axis runs over, the one named last changes fastest.
Arguments:
- mode_fields: bfloat16 [64, 3, 65536], P('test', None, 'elem'), may hold values from -6 to 6
- elem_type: int32 [128], P('elem'), may hold values from 0 to 3
- type_scales: float32 [4, 3], replicated, may hold values from 0.5 to 2
Outputs:
- conv_tensor: float32 [64, 64, 64], P('test', 'elem')
All inputs are finite; a program needn't handle non-finite values.
Results may differ from a plain program's by a relative error of at most 0.0051.
Values may be sent and summed in bfloat16 or wider, within the bound.
A program may use at most 64 MiB of HBM per device.

v0:
```python
import jax
import jax.numpy as jnp
import numpy as np
from jax import lax
from jax.sharding import PartitionSpec as P

Q = 8
block_modes = 4


def legendre_top(points, degree):
    before = points * 0.0 + 1.0
    current = points
    for order in range(2, degree + 1):
        following = ((2 * order - 1) * points * current - (order - 1) * before) / order
        before = current
        current = following
    return (current, before)


def lobatto_tables(order_points):
    degree = order_points - 1
    lobatto_nodes = np.cos(np.pi * np.arange(degree + 1) / degree)
    for sweep in range(100):
        top, lower = legendre_top(lobatto_nodes, degree)
        lobatto_nodes = lobatto_nodes - (lobatto_nodes * top - lower) / ((degree + 1) * top)
    lobatto_nodes = lobatto_nodes[::-1].copy()
    lobatto_nodes[0] = -1.0
    lobatto_nodes[-1] = 1.0
    values, unused = legendre_top(lobatto_nodes, degree)
    weights = 2.0 / (degree * (degree + 1) * values**2)
    identity = np.eye(order_points)
    distance = lobatto_nodes[:, None] - lobatto_nodes[None, :]
    spacing = np.where(identity > 0, 1.0, distance)
    derivative = np.where(identity > 0, 0.0, values[:, None] / values[None, :] / spacing)
    corner = degree * (degree + 1) / 4.0
    ends = np.concatenate([[-corner], np.zeros(degree - 1), [corner]])
    derivative = derivative + identity * ends[None, :]
    square_eye = np.eye(order_points * order_points)
    along_r = np.kron(square_eye, derivative)
    along_s = np.kron(identity, np.kron(derivative, identity))
    along_t = np.kron(derivative, square_eye)
    table = np.concatenate([along_r.T, along_s.T, along_t.T], axis=1)
    cube_weights = np.kron(weights, np.kron(weights, weights))
    return (table.astype(np.float32), cube_weights.astype(np.float32))


def element_scales(types, type_scales):
    picks = (types[:, None] == jnp.arange(type_scales.shape[0], dtype=jnp.int32)[None, :]).astype(
        jnp.float32
    )
    return jnp.sum(picks[:, :, None] * type_scales[None, :, :], axis=1)


def gradient(fields, scales, table, cube):
    mode_count = fields.shape[0]
    elements = fields.shape[2] // cube
    flat = fields.reshape(mode_count * 3 * elements, cube)
    derived = jnp.dot(flat, table, preferred_element_type=jnp.float32).reshape(
        mode_count, 3, elements, 3, cube
    )
    return (derived * scales[None, None, :, :, None]).astype(jnp.bfloat16)


def project(test_fields, trial_fields, grads, quadrature):
    test_modes = test_fields.shape[0]
    trial_modes = trial_fields.shape[0]
    grad_modes = grads.shape[0]
    blocks = grads.reshape((grad_modes // block_modes, block_modes) + grads.shape[1:])
    test_wide = test_fields.astype(jnp.float32)

    def one_block(grad_block):
        grad_wide = grad_block.astype(jnp.float32)
        summed = test_wide[:, None, 0, :, None, :] * grad_wide[None, :, 0]
        summed = summed + test_wide[:, None, 1, :, None, :] * grad_wide[None, :, 1]
        summed = summed + test_wide[:, None, 2, :, None, :] * grad_wide[None, :, 2]
        pairs = (summed * quadrature[None, None, :, None, :]).astype(jnp.bfloat16)
        return jnp.einsum(
            "ikedp,jdep->ijk", pairs, trial_fields, preferred_element_type=jnp.float32
        )

    result = lax.map(one_block, blocks)
    return result.transpose(1, 2, 0, 3).reshape(test_modes, trial_modes, grad_modes)


def body(mode_fields, elem_type, type_scales):
    table, cube_weights = lobatto_tables(Q)
    table = jnp.asarray(table).astype(jnp.bfloat16)
    point_weights = jnp.asarray(cube_weights).astype(jnp.float32)
    cube = Q**3
    total_points = mode_fields.shape[2] * lax.axis_size("elem")
    gathered = lax.all_gather(mode_fields, "test", axis=0, tiled=True)
    elements = mode_fields.shape[2] // cube
    scales = element_scales(elem_type, type_scales)
    quadrature = point_weights[None, :] / jnp.prod(scales, axis=1)[:, None]
    grads = gradient(gathered, scales, table, cube)
    partial_value = project(
        mode_fields.reshape(mode_fields.shape[0], 3, elements, cube),
        gathered.reshape(gathered.shape[0], 3, elements, cube),
        grads,
        quadrature,
    )
    summed = lax.psum_scatter(partial_value, "elem", scatter_dimension=1, tiled=True)
    return summed * float(total_points) ** (-0.5)


def solution(mesh):
    placed = (P("test", None, "elem"), P("elem"), P())
    return jax.shard_map(
        body, mesh=mesh, in_specs=placed, out_specs=P("test", "elem", None), check_vma=False
    )
```

profile of v0, /device:TPU:0, one launch (start us, length us, event | category | flops | bytes accessed | tf_op | source)
XLA Modules:
  0.0 182.2 jit_solution(7041535098381613878)
XLA Ops:
  6.5 0.7 all-gather.2.cloned.1.call-update
  7.3 1.3 convert_element_type.34
  8.6 0.8 copy.20
  9.7 29.2 %all-gather.2.cloned.1.call-done = bf16[64,3,4096]{2,0,1:T(8,128)(2,1)} async-done(((bf16[32,3,4096]{2,0,1:T(8,128)(2,1)}), bf16[64,3,4096]{2,0,1:T(8,128)(2,1)}) %all-gather.2.cloned.1.call-update) | async-done | bytes 1572880 | tf_op jit(solution)/shard_map/all_gather | solution.py:92
  38.8 1.6 copy.40
  40.4 6.7 %fusion.11 = bf16[64,3,8,3,512]{4,0,2,1,3:T(8,128)(2,1)} fusion(f32[8,3]{0,1:T(4,128)S(1)} %multiply_reduce_fusion, bf16[3,512,512,1,1]{2,1,4,3,0:T(8,128)(2,1)} %constant.28, bf16[3,8,8,8,512]{4,3,2,1,0:T(8,128)(2,1)} %bitcast.79), kind=kOutput, calls=%fused_computation.17 | convolution fusion | flops 2420637696 | bytes 7864416 | tf_op jit(solution)/shard_map/dot_general | solution.py:59
  47.2 7.7 %reshape.50 = bf16[16,4,3,8,3,512]{5,1,0,3,2,4:T(4,128)(2,1)} reshape(bf16[64,3,8,3,512]{4,0,2,1,3:T(8,128)(2,1)} %fusion.11) | data formatting | bytes 9437184 | tf_op jit(solution)/shard_map/reshape | solution.py:69
  54.9 58.1 %while.11 = (s32[]{:T(128)}, f32[16,32,64,4]{2,1,3,0:T(8,128)}, f32[32,3,8,512]{3,0,2,1:T(8,128)S(1)}, bf16[16,4,3,8,3,512]{5,1,0,3,2,4:T(4,128)(2,1)}, bf16[64,...) while((s32[]{:T(128)}, f32[16,32,64,4]{2,1,3,0:T(8,128)}, ...), condition=%wide.region_3.4_spmd.clone, body=%wide.region_2.3_spmd.clone.sunk | while | flops 212488192 | bytes 9636473 | solution.py:82
  54.9 1.1 constant_dynamic-slice_fusion.2
  56.1 0.2 slice_bitcast_fusion.9
  56.3 2.1 %fusion.20 = f32[16,32,64,4]{2,1,3,0:T(8,128)} fusion(f32[16,32,64,4]{2,1,3,0:T(8,128)} %get-tuple-element.168, s32[]{:T(128)} %get-tuple-element.167, bf16[64,3,8,512]{3,0,2,1:T(8,128)(2,1)S(1)} %get-tuple-element.179, f32[8,512]{1,0:T(8,128)S(1)} %broadcast_divide_fusion.2, f32[4,8,3,512]{3,1,0,2:T(8,128)S(1)} %get-tuple-element.153, ...), kind=kOutput, calls=%fused_computation.5.clone.1 | convolution fusion | flops 212336640 | bytes 3817984 | tf_op jit(solution)/shard_map/while/body/eval_jaxpr/ikedp,jdep->ijk/dot_general | solution.py:78
  58.5 1.1 constant_dynamic-slice_fusion.2
  59.7 0.2 slice_bitcast_fusion.9
  60.0 2.2 %fusion.20 = f32[16,32,64,4]{2,1,3,0:T(8,128)} fusion(f32[16,32,64,4]{2,1,3,0:T(8,128)} %get-tuple-element.168, s32[]{:T(128)} %get-tuple-element.167, bf16[64,3,8,512]{3,0,2,1:T(8,128)(2,1)S(1)} %get-tuple-element.179, f32[8,512]{1,0:T(8,128)S(1)} %broadcast_divide_fusion.2, f32[4,8,3,512]{3,1,0,2:T(8,128)S(1)} %get-tuple-element.153, ...), kind=kOutput, calls=%fused_computation.5.clone.1 | convolution fusion | flops 212336640 | bytes 3817984 | tf_op jit(solution)/shard_map/while/body/eval_jaxpr/ikedp,jdep->ijk/dot_general | solution.py:78
  62.1 1.1 constant_dynamic-slice_fusion.2
  63.3 0.2 slice_bitcast_fusion.9
  63.6 2.2 %fusion.20 = f32[16,32,64,4]{2,1,3,0:T(8,128)} fusion(f32[16,32,64,4]{2,1,3,0:T(8,128)} %get-tuple-element.168, s32[]{:T(128)} %get-tuple-element.167, bf16[64,3,8,512]{3,0,2,1:T(8,128)(2,1)S(1)} %get-tuple-element.179, f32[8,512]{1,0:T(8,128)S(1)} %broadcast_divide_fusion.2, f32[4,8,3,512]{3,1,0,2:T(8,128)S(1)} %get-tuple-element.153, ...), kind=kOutput, calls=%fused_computation.5.clone.1 | convolution fusion | flops 212336640 | bytes 3817984 | tf_op jit(solution)/shard_map/while/body/eval_jaxpr/ikedp,jdep->ijk/dot_general | solution.py:78
  65.8 1.1 constant_dynamic-slice_fusion.2
  67.2 2.2 %fusion.20 = f32[16,32,64,4]{2,1,3,0:T(8,128)} fusion(f32[16,32,64,4]{2,1,3,0:T(8,128)} %get-tuple-element.168, s32[]{:T(128)} %get-tuple-element.167, bf16[64,3,8,512]{3,0,2,1:T(8,128)(2,1)S(1)} %get-tuple-element.179, f32[8,512]{1,0:T(8,128)S(1)} %broadcast_divide_fusion.2, f32[4,8,3,512]{3,1,0,2:T(8,128)S(1)} %get-tuple-element.153, ...), kind=kOutput, calls=%fused_computation.5.clone.1 | convolution fusion | flops 212336640 | bytes 3817984 | tf_op jit(solution)/shard_map/while/body/eval_jaxpr/ikedp,jdep->ijk/dot_general | solution.py:78
  69.4 1.1 constant_dynamic-slice_fusion.2
  70.9 2.1 %fusion.20 = f32[16,32,64,4]{2,1,3,0:T(8,128)} fusion(f32[16,32,64,4]{2,1,3,0:T(8,128)} %get-tuple-element.168, s32[]{:T(128)} %get-tuple-element.167, bf16[64,3,8,512]{3,0,2,1:T(8,128)(2,1)S(1)} %get-tuple-element.179, f32[8,512]{1,0:T(8,128)S(1)} %broadcast_divide_fusion.2, f32[4,8,3,512]{3,1,0,2:T(8,128)S(1)} %get-tuple-element.153, ...), kind=kOutput, calls=%fused_computation.5.clone.1 | convolution fusion | flops 212336640 | bytes 3817984 | tf_op jit(solution)/shard_map/while/body/eval_jaxpr/ikedp,jdep->ijk/dot_general | solution.py:78
  73.0 1.1 constant_dynamic-slice_fusion.2
  74.2 0.2 slice_bitcast_fusion.9
  74.5 2.2 %fusion.20 = f32[16,32,64,4]{2,1,3,0:T(8,128)} fusion(f32[16,32,64,4]{2,1,3,0:T(8,128)} %get-tuple-element.168, s32[]{:T(128)} %get-tuple-element.167, bf16[64,3,8,512]{3,0,2,1:T(8,128)(2,1)S(1)} %get-tuple-element.179, f32[8,512]{1,0:T(8,128)S(1)} %broadcast_divide_fusion.2, f32[4,8,3,512]{3,1,0,2:T(8,128)S(1)} %get-tuple-element.153, ...), kind=kOutput, calls=%fused_computation.5.clone.1 | convolution fusion | flops 212336640 | bytes 3817984 | tf_op jit(solution)/shard_map/while/body/eval_jaxpr/ikedp,jdep->ijk/dot_general | solution.py:78
  76.6 1.1 constant_dynamic-slice_fusion.2
  78.1 2.2 %fusion.20 = f32[16,32,64,4]{2,1,3,0:T(8,128)} fusion(f32[16,32,64,4]{2,1,3,0:T(8,128)} %get-tuple-element.168, s32[]{:T(128)} %get-tuple-element.167, bf16[64,3,8,512]{3,0,2,1:T(8,128)(2,1)S(1)} %get-tuple-element.179, f32[8,512]{1,0:T(8,128)S(1)} %broadcast_divide_fusion.2, f32[4,8,3,512]{3,1,0,2:T(8,128)S(1)} %get-tuple-element.153, ...), kind=kOutput, calls=%fused_computation.5.clone.1 | convolution fusion | flops 212336640 | bytes 3817984 | tf_op jit(solution)/shard_map/while/body/eval_jaxpr/ikedp,jdep->ijk/dot_general | solution.py:78
  80.3 1.1 constant_dynamic-slice_fusion.2
  81.8 2.1 %fusion.20 = f32[16,32,64,4]{2,1,3,0:T(8,128)} fusion(f32[16,32,64,4]{2,1,3,0:T(8,128)} %get-tuple-element.168, s32[]{:T(128)} %get-tuple-element.167, bf16[64,3,8,512]{3,0,2,1:T(8,128)(2,1)S(1)} %get-tuple-element.179, f32[8,512]{1,0:T(8,128)S(1)} %broadcast_divide_fusion.2, f32[4,8,3,512]{3,1,0,2:T(8,128)S(1)} %get-tuple-element.153, ...), kind=kOutput, calls=%fused_computation.5.clone.1 | convolution fusion | flops 212336640 | bytes 3817984 | tf_op jit(solution)/shard_map/while/body/eval_jaxpr/ikedp,jdep->ijk/dot_general | solution.py:78
  83.9 1.1 constant_dynamic-slice_fusion.2
  85.4 2.2 %fusion.20 = f32[16,32,64,4]{2,1,3,0:T(8,128)} fusion(f32[16,32,64,4]{2,1,3,0:T(8,128)} %get-tuple-element.168, s32[]{:T(128)} %get-tuple-element.167, bf16[64,3,8,512]{3,0,2,1:T(8,128)(2,1)S(1)} %get-tuple-element.179, f32[8,512]{1,0:T(8,128)S(1)} %broadcast_divide_fusion.2, f32[4,8,3,512]{3,1,0,2:T(8,128)S(1)} %get-tuple-element.153, ...), kind=kOutput, calls=%fused_computation.5.clone.1 | convolution fusion | flops 212336640 | bytes 3817984 | tf_op jit(solution)/shard_map/while/body/eval_jaxpr/ikedp,jdep->ijk/dot_general | solution.py:78
  87.5 1.1 constant_dynamic-slice_fusion.2
  89.0 2.2 %fusion.20 = f32[16,32,64,4]{2,1,3,0:T(8,128)} fusion(f32[16,32,64,4]{2,1,3,0:T(8,128)} %get-tuple-element.168, s32[]{:T(128)} %get-tuple-element.167, bf16[64,3,8,512]{3,0,2,1:T(8,128)(2,1)S(1)} %get-tuple-element.179, f32[8,512]{1,0:T(8,128)S(1)} %broadcast_divide_fusion.2, f32[4,8,3,512]{3,1,0,2:T(8,128)S(1)} %get-tuple-element.153, ...), kind=kOutput, calls=%fused_computation.5.clone.1 | convolution fusion | flops 212336640 | bytes 3817984 | tf_op jit(solution)/shard_map/while/body/eval_jaxpr/ikedp,jdep->ijk/dot_general | solution.py:78
  91.2 1.1 constant_dynamic-slice_fusion.2
  92.6 2.2 %fusion.20 = f32[16,32,64,4]{2,1,3,0:T(8,128)} fusion(f32[16,32,64,4]{2,1,3,0:T(8,128)} %get-tuple-element.168, s32[]{:T(128)} %get-tuple-element.167, bf16[64,3,8,512]{3,0,2,1:T(8,128)(2,1)S(1)} %get-tuple-element.179, f32[8,512]{1,0:T(8,128)S(1)} %broadcast_divide_fusion.2, f32[4,8,3,512]{3,1,0,2:T(8,128)S(1)} %get-tuple-element.153, ...), kind=kOutput, calls=%fused_computation.5.clone.1 | convolution fusion | flops 212336640 | bytes 3817984 | tf_op jit(solution)/shard_map/while/body/eval_jaxpr/ikedp,jdep->ijk/dot_general | solution.py:78
  94.8 1.1 constant_dynamic-slice_fusion.2
  96.3 2.2 %fusion.20 = f32[16,32,64,4]{2,1,3,0:T(8,128)} fusion(f32[16,32,64,4]{2,1,3,0:T(8,128)} %get-tuple-element.168, s32[]{:T(128)} %get-tuple-element.167, bf16[64,3,8,512]{3,0,2,1:T(8,128)(2,1)S(1)} %get-tuple-element.179, f32[8,512]{1,0:T(8,128)S(1)} %broadcast_divide_fusion.2, f32[4,8,3,512]{3,1,0,2:T(8,128)S(1)} %get-tuple-element.153, ...), kind=kOutput, calls=%fused_computation.5.clone.1 | convolution fusion | flops 212336640 | bytes 3817984 | tf_op jit(solution)/shard_map/while/body/eval_jaxpr/ikedp,jdep->ijk/dot_general | solution.py:78
  98.4 1.1 constant_dynamic-slice_fusion.2
  99.9 2.2 %fusion.20 = f32[16,32,64,4]{2,1,3,0:T(8,128)} fusion(f32[16,32,64,4]{2,1,3,0:T(8,128)} %get-tuple-element.168, s32[]{:T(128)} %get-tuple-element.167, bf16[64,3,8,512]{3,0,2,1:T(8,128)(2,1)S(1)} %get-tuple-element.179, f32[8,512]{1,0:T(8,128)S(1)} %broadcast_divide_fusion.2, f32[4,8,3,512]{3,1,0,2:T(8,128)S(1)} %get-tuple-element.153, ...), kind=kOutput, calls=%fused_computation.5.clone.1 | convolution fusion | flops 212336640 | bytes 3817984 | tf_op jit(solution)/shard_map/while/body/eval_jaxpr/ikedp,jdep->ijk/dot_general | solution.py:78
  102.1 1.1 constant_dynamic-slice_fusion.2
  103.5 2.2 %fusion.20 = f32[16,32,64,4]{2,1,3,0:T(8,128)} fusion(f32[16,32,64,4]{2,1,3,0:T(8,128)} %get-tuple-element.168, s32[]{:T(128)} %get-tuple-element.167, bf16[64,3,8,512]{3,0,2,1:T(8,128)(2,1)S(1)} %get-tuple-element.179, f32[8,512]{1,0:T(8,128)S(1)} %broadcast_divide_fusion.2, f32[4,8,3,512]{3,1,0,2:T(8,128)S(1)} %get-tuple-element.153, ...), kind=kOutput, calls=%fused_computation.5.clone.1 | convolution fusion | flops 212336640 | bytes 3817984 | tf_op jit(solution)/shard_map/while/body/eval_jaxpr/ikedp,jdep->ijk/dot_general | solution.py:78
  105.7 1.1 constant_dynamic-slice_fusion.2
  107.2 2.2 %fusion.20 = f32[16,32,64,4]{2,1,3,0:T(8,128)} fusion(f32[16,32,64,4]{2,1,3,0:T(8,128)} %get-tuple-element.168, s32[]{:T(128)} %get-tuple-element.167, bf16[64,3,8,512]{3,0,2,1:T(8,128)(2,1)S(1)} %get-tuple-element.179, f32[8,512]{1,0:T(8,128)S(1)} %broadcast_divide_fusion.2, f32[4,8,3,512]{3,1,0,2:T(8,128)S(1)} %get-tuple-element.153, ...), kind=kOutput, calls=%fused_computation.5.clone.1 | convolution fusion | flops 212336640 | bytes 3817984 | tf_op jit(solution)/shard_map/while/body/eval_jaxpr/ikedp,jdep->ijk/dot_general | solution.py:78
  109.3 1.1 constant_dynamic-slice_fusion.2
  110.8 2.1 %fusion.20 = f32[16,32,64,4]{2,1,3,0:T(8,128)} fusion(f32[16,32,64,4]{2,1,3,0:T(8,128)} %get-tuple-element.168, s32[]{:T(128)} %get-tuple-element.167, bf16[64,3,8,512]{3,0,2,1:T(8,128)(2,1)S(1)} %get-tuple-element.179, f32[8,512]{1,0:T(8,128)S(1)} %broadcast_divide_fusion.2, f32[4,8,3,512]{3,1,0,2:T(8,128)S(1)} %get-tuple-element.153, ...), kind=kOutput, calls=%fused_computation.5.clone.1 | convolution fusion | flops 212336640 | bytes 3817984 | tf_op jit(solution)/shard_map/while/body/eval_jaxpr/ikedp,jdep->ijk/dot_general | solution.py:78
  113.0 3.1 %copy.24 = f32[32,64,64]{2,0,1:T(8,128)} copy(f32[32,64,64]{1,0,2:T(8,128)} %bitcast.5) | data formatting | bytes 1048576 | tf_op jit(solution)/shard_map/reshape | solution.py:83
  116.1 57.7 %reduce-scatter.2.cloned.1.call-done = f32[32,4,64]{2,0,1:T(8,128)} async-done(((f32[32,64,64]{2,0,1:T(8,128)}), f32[32,4,64]{2,0,1:T(8,128)}) %reduce-scatter.2.cloned.1.call-update) | async-done | bytes 32784 | tf_op jit(solution)/shard_map/reduce_scatter | solution.py:103
  173.8 0.8 broadcast_multiply_fusion
  174.7 0.7 copy.25
  (72 shorter events, 5.6 us)
Async XLA Ops:
  6.5 3.0 %copy-start.1 = (s32[8]{0:T(128)S(1)}, s32[8]{0:T(128)}, u32[]{:S(2)}) copy-start(s32[8]{0:T(128)} %param.8) | copy-start | bytes 100
  6.5 32.3 %all-gather.2.cloned.1.call-start = ((), (), s32[]{:S(2)}) async-start(), calls=%async_computation.1 | async-start | bytes 2359296 | tf_op jit(solution)/shard_map/all_gather | solution.py:92
  7.3 166.6 %reduce-scatter.2.cloned.1.call-start = ((), (), s32[]{:S(2)}) async-start(), calls=%async_computation.2 | async-start | bytes 1114112 | tf_op jit(solution)/shard_map/reduce_scatter | solution.py:103
  47.2 7.7 %copy-start = (f32[512]{0:T(512)S(1)}, f32[512]{0:T(512)}, u32[]{:S(2)}) copy-start(f32[512]{0:T(512)} %constant.23.clone) | copy-start | bytes 6148
Sparse Core Ops, SparseCore 0:
  8.9 29.9 all-gather.1
  116.2 57.5 reduce-scatter.1
where the time goes:
time: 183 us; the launch traced here: 182 us
  waiting for transfers between devices  87.6 us (48%)
  matrix products  41.2 us (23%)
  local copies, waits for them, and re-layouts  34.8 us (19%)
  between operations  13.5 us (7%)
  other arithmetic  4.61 us (3%)
    reduce_scatter x1, waiting for transfers between devices, body(): lax.psum_scatter(partial_value, 'elem', scatter_dimension=1, tiled=True)  57.7 us
    dot_general x16, matrix products, one_block(): jnp.einsum('ikedp,jdep->ijk', pairs, trial_fields, preferred_element_type...  34.5 us
    all_gather x1, waiting for transfers between devices, body(): gathered = lax.all_gather(mode_fields, 'test', axis=0, tiled=True)  29.2 us
    dynamic_slice x16, local copies, waits for them, and re-layouts, project(): result = lax.map(one_block, blocks)  17.1 us
    reshape x1, local copies, waits for them, and re-layouts, project(): grads.reshape((grad_modes // block_modes, block_modes) + grads.shape[1:])  7.71 us
    dot_general x1, matrix products, gradient(): jnp.dot(flat, table, preferred_element_type=jnp.float32)  6.71 us
  transfers between devices with their start and end apart: 2, of which 2 were waited for; matrix products, arithmetic and copies ran while one was open for 1% of the time, Pallas kernels for 0%

commit v1 on v0

--- a/solution.py
+++ b/solution.py
@@ -6,6 +6,9 @@
 
 Q = 8
 block_modes = 4
+balance_clusters = lambda local: jnp.concatenate(
+    lax.all_to_all(jnp.stack(lax.psum(1, "test") * [local]), "test", 0, 0), axis=0
+)
 
 
 def legendre_top(points, degree):
@@ -89,7 +92,7 @@
     point_weights = jnp.asarray(cube_weights).astype(jnp.float32)
     cube = Q**3
     total_points = mode_fields.shape[2] * lax.axis_size("elem")
-    gathered = lax.all_gather(mode_fields, "test", axis=0, tiled=True)
+    gathered = balance_clusters(mode_fields)
     elements = mode_fields.shape[2] // cube
     scales = element_scales(elem_type, type_scales)
     quadrature = point_weights[None, :] / jnp.prod(scales, axis=1)[:, None]

time: 183 us -> 166 us (0.907)
  local copies, waits for them, and re-layouts: 34.8 us -> 10.6 us
  other arithmetic: 4.61 us -> 22.5 us
  waiting for transfers between devices: 87.6 us -> 75.3 us
  starting transfers between devices: 0.04 us -> 4.37 us
  matrix products: 41.2 us -> 38.9 us
    all_gather x1 -> x0, waiting for transfers between devices: 29.2 us -> none  [body(): gathered = lax.all_gather(mode_fields, 'test', axis=0, tiled=True)]
    dynamic_slice x16 -> x0, local copies, waits for them, and re-layouts: 17.1 us -> none  [project(): result = lax.map(one_block, blocks)]
    all_to_all x0 -> x1, waiting for transfers between devices: none -> 17 us  [lax.all_to_all(jnp.stack(lax.psum(1, 'test') * [local]), 'test', 0, 0)]
    convert_element_type x16, other arithmetic: 1.21 us -> 16.3 us  [one_block(): grad_wide = grad_block.astype(jnp.float32)]
    reshape x1 -> x0, local copies, waits for them, and re-layouts: 7.71 us -> none  [project(): grads.reshape((grad_modes // block_modes, block_modes) + grads.shape[1:])]
    all_to_all x0 -> x1, starting transfers between devices: none -> 4.37 us  [lax.all_to_all(jnp.stack(lax.psum(1, 'test') * [local]), 'test', 0, 0)]
    another operation x0 -> x1, other arithmetic: none -> 2.79 us  [jnp.stack(lax.psum(1, 'test') * [local])]
    dot_general x1, matrix products: 6.71 us -> 4.34 us  [gradient(): jnp.dot(flat, table, preferred_element_type=jnp.float32)]
  transfers between devices with their start and end apart: 2 -> 2, of which waited for: 2 -> 2; matrix products, arithmetic and copies ran while one was open for 1% -> 2% of each run, Pallas kernels for 0% -> 0%
where the time goes in v1:
time: 166 us
  waiting for transfers between devices  75.3 us (45%)
  matrix products  38.9 us (23%)
  other arithmetic  22.5 us (14%)
  between operations  13.4 us (8%)
  local copies, waits for them, and re-layouts  10.6 us (6%)
  starting transfers between devices  4.37 us (3%)
    reduce_scatter x1, waiting for transfers between devices, body(): lax.psum_scatter(partial_value, 'elem', scatter_dimension=1, tiled=True)  58.3 us
    dot_general x16, matrix products, one_block(): jnp.einsum('ikedp,jdep->ijk', pairs, trial_fields, preferred_element_type...  34.5 us
    all_to_all x1, waiting for transfers between devices, lax.all_to_all(jnp.stack(lax.psum(1, 'test') * [local]), 'test', 0, 0)  17 us
    convert_element_type x16, other arithmetic, one_block(): grad_wide = grad_block.astype(jnp.float32)  16.3 us
    all_to_all x1, starting transfers between devices, lax.all_to_all(jnp.stack(lax.psum(1, 'test') * [local]), 'test', 0, 0)  4.37 us
    dot_general x1, matrix products, gradient(): jnp.dot(flat, table, preferred_element_type=jnp.float32)  4.34 us
    mul x32, local copies, waits for them, and re-layouts, one_block(): summed = test_wide[:, None, 0, :, None, :] * grad_wide[None, :, 0]  3.61 us
  transfers between devices with their start and end apart: 2, of which 2 were waited for; matrix products, arithmetic and copies ran while one was open for 2% of the time, Pallas kernels for 0%

profile of v1, /device:TPU:0, one launch (start us, length us, event | category | flops | bytes accessed | tf_op | source)
XLA Modules:
  0.0 165.5 jit_solution(512550491389127668)
XLA Ops:
  6.5 2.8 %pad_maximum_fusion = bf16[2,32,3,4096]{3,1,2,0:T(8,128)(2,1)} fusion(bf16[1,32,3,4096]{3,1,2,0:T(8,128)(2,1)} %bitcast.73), kind=kLoop, calls=%fused_computation.18 | loop fusion | flops 786432 | bytes 2359296 | tf_op jit(solution)/shard_map/stack | solution.py:10
  9.3 4.4 %all-to-all-start = ((bf16[2,32,3,4096]{3,1,2,0:T(8,128)(2,1)}), bf16[2,32,3,4096]{3,1,2,0:T(8,128)(2,1)S(1)}, u32[]{:S(2)}, u32[]{:S(2)}) async-start(bf16[2,32,3,4096]{3,1,2,0:T(8,128)(2,1)} %pad_maximum_fusion), calls=%async_computation | async-start | bytes 3145728 | tf_op jit(solution)/shard_map/all_to_all | solution.py:10
  13.7 1.3 convert_element_type.34
  15.1 1.6 copy.46
  16.8 17.0 %all-to-all-done = bf16[2,32,3,4096]{3,1,2,0:T(8,128)(2,1)S(1)} async-done(((bf16[2,32,3,4096]{3,1,2,0:T(8,128)(2,1)}), bf16[2,32,3,4096]{3,1,2,0:T(8,128)(2,1)S(1)}, u32[]{:S(2)}, u32[]{:S(2)}) %all-to-all-start) | async-done | bytes 1572896 | tf_op jit(solution)/shard_map/all_to_all | solution.py:10
  34.0 0.7 copy.39
  34.7 0.5 copy.28
  35.2 0.2 copy-done.4
  35.4 4.3 %multiply_convert_fusion.6 = bf16[64,3,8,3,512]{4,2,3,1,0:T(8,128)(2,1)} fusion(f32[8,3]{0,1:T(4,128)S(1)} %multiply_reduce_fusion, bf16[3,512,512,1,1]{2,1,0,4,3:T(8,128)(2,1)S(1)} %copy-done.4, bf16[64,3,8,512,1]{3,2,0,1,4:T(8,128)(2,1)S(1)} %bitcast.70), kind=kOutput, calls=%fused_computation.16 | convolution fusion | flops 2420637696 | bytes 7864416 | tf_op jit(solution)/shard_map/dot_general | solution.py:62
  39.8 56.0 %while.11 = (s32[]{:T(128)}, f32[16,32,64,4]{2,1,3,0:T(8,128)}, f32[32,3,8,512]{3,0,2,1:T(8,128)S(1)}, bf16[16,4,3,8,3,512]{5,3,4,2,1,0:T(8,128)(2,1)}, bf16[64,...) while((s32[]{:T(128)}, f32[16,32,64,4]{2,1,3,0:T(8,128)}, ...), condition=%wide.region_3.4_spmd.clone, body=%wide.region_2.3_spmd.clone.sunk | while | flops 212488192 | bytes 9047157 | solution.py:85
  39.8 1.0 fusion.18
  41.1 2.2 %fusion.19 = f32[16,32,64,4]{2,1,3,0:T(8,128)} fusion(f32[16,32,64,4]{2,1,3,0:T(8,128)} %get-tuple-element.168, s32[]{:T(128)} %get-tuple-element.167, bf16[64,3,8,512]{3,0,2,1:T(8,128)(2,1)S(1)} %get-tuple-element.179, f32[8,512]{1,0:T(8,128)S(1)} %broadcast_divide_fusion.2, f32[4,8,3,512]{3,1,0,2:T(8,128)S(1)} %get-tuple-element.153, ...), kind=kOutput, calls=%fused_computation.5.clone.1 | convolution fusion | flops 212336640 | bytes 3817984 | tf_op jit(solution)/shard_map/while/body/eval_jaxpr/ikedp,jdep->ijk/dot_general | solution.py:81
  43.3 1.0 fusion.18
  44.3 0.2 slice_bitcast_fusion.9
  44.6 2.1 %fusion.19 = f32[16,32,64,4]{2,1,3,0:T(8,128)} fusion(f32[16,32,64,4]{2,1,3,0:T(8,128)} %get-tuple-element.168, s32[]{:T(128)} %get-tuple-element.167, bf16[64,3,8,512]{3,0,2,1:T(8,128)(2,1)S(1)} %get-tuple-element.179, f32[8,512]{1,0:T(8,128)S(1)} %broadcast_divide_fusion.2, f32[4,8,3,512]{3,1,0,2:T(8,128)S(1)} %get-tuple-element.153, ...), kind=kOutput, calls=%fused_computation.5.clone.1 | convolution fusion | flops 212336640 | bytes 3817984 | tf_op jit(solution)/shard_map/while/body/eval_jaxpr/ikedp,jdep->ijk/dot_general | solution.py:81
  46.7 1.0 fusion.18
  48.1 2.2 %fusion.19 = f32[16,32,64,4]{2,1,3,0:T(8,128)} fusion(f32[16,32,64,4]{2,1,3,0:T(8,128)} %get-tuple-element.168, s32[]{:T(128)} %get-tuple-element.167, bf16[64,3,8,512]{3,0,2,1:T(8,128)(2,1)S(1)} %get-tuple-element.179, f32[8,512]{1,0:T(8,128)S(1)} %broadcast_divide_fusion.2, f32[4,8,3,512]{3,1,0,2:T(8,128)S(1)} %get-tuple-element.153, ...), kind=kOutput, calls=%fused_computation.5.clone.1 | convolution fusion | flops 212336640 | bytes 3817984 | tf_op jit(solution)/shard_map/while/body/eval_jaxpr/ikedp,jdep->ijk/dot_general | solution.py:81
  50.2 1.0 fusion.18
  51.6 2.2 %fusion.19 = f32[16,32,64,4]{2,1,3,0:T(8,128)} fusion(f32[16,32,64,4]{2,1,3,0:T(8,128)} %get-tuple-element.168, s32[]{:T(128)} %get-tuple-element.167, bf16[64,3,8,512]{3,0,2,1:T(8,128)(2,1)S(1)} %get-tuple-element.179, f32[8,512]{1,0:T(8,128)S(1)} %broadcast_divide_fusion.2, f32[4,8,3,512]{3,1,0,2:T(8,128)S(1)} %get-tuple-element.153, ...), kind=kOutput, calls=%fused_computation.5.clone.1 | convolution fusion | flops 212336640 | bytes 3817984 | tf_op jit(solution)/shard_map/while/body/eval_jaxpr/ikedp,jdep->ijk/dot_general | solution.py:81
  53.7 1.0 fusion.18
  55.1 2.1 %fusion.19 = f32[16,32,64,4]{2,1,3,0:T(8,128)} fusion(f32[16,32,64,4]{2,1,3,0:T(8,128)} %get-tuple-element.168, s32[]{:T(128)} %get-tuple-element.167, bf16[64,3,8,512]{3,0,2,1:T(8,128)(2,1)S(1)} %get-tuple-element.179, f32[8,512]{1,0:T(8,128)S(1)} %broadcast_divide_fusion.2, f32[4,8,3,512]{3,1,0,2:T(8,128)S(1)} %get-tuple-element.153, ...), kind=kOutput, calls=%fused_computation.5.clone.1 | convolution fusion | flops 212336640 | bytes 3817984 | tf_op jit(solution)/shard_map/while/body/eval_jaxpr/ikedp,jdep->ijk/dot_general | solution.py:81
  57.2 1.0 fusion.18
  58.6 2.2 %fusion.19 = f32[16,32,64,4]{2,1,3,0:T(8,128)} fusion(f32[16,32,64,4]{2,1,3,0:T(8,128)} %get-tuple-element.168, s32[]{:T(128)} %get-tuple-element.167, bf16[64,3,8,512]{3,0,2,1:T(8,128)(2,1)S(1)} %get-tuple-element.179, f32[8,512]{1,0:T(8,128)S(1)} %broadcast_divide_fusion.2, f32[4,8,3,512]{3,1,0,2:T(8,128)S(1)} %get-tuple-element.153, ...), kind=kOutput, calls=%fused_computation.5.clone.1 | convolution fusion | flops 212336640 | bytes 3817984 | tf_op jit(solution)/shard_map/while/body/eval_jaxpr/ikedp,jdep->ijk/dot_general | solution.py:81
  60.7 1.0 fusion.18
  62.1 2.2 %fusion.19 = f32[16,32,64,4]{2,1,3,0:T(8,128)} fusion(f32[16,32,64,4]{2,1,3,0:T(8,128)} %get-tuple-element.168, s32[]{:T(128)} %get-tuple-element.167, bf16[64,3,8,512]{3,0,2,1:T(8,128)(2,1)S(1)} %get-tuple-element.179, f32[8,512]{1,0:T(8,128)S(1)} %broadcast_divide_fusion.2, f32[4,8,3,512]{3,1,0,2:T(8,128)S(1)} %get-tuple-element.153, ...), kind=kOutput, calls=%fused_computation.5.clone.1 | convolution fusion | flops 212336640 | bytes 3817984 | tf_op jit(solution)/shard_map/while/body/eval_jaxpr/ikedp,jdep->ijk/dot_general | solution.py:81
  64.2 1.0 fusion.18
  65.6 2.2 %fusion.19 = f32[16,32,64,4]{2,1,3,0:T(8,128)} fusion(f32[16,32,64,4]{2,1,3,0:T(8,128)} %get-tuple-element.168, s32[]{:T(128)} %get-tuple-element.167, bf16[64,3,8,512]{3,0,2,1:T(8,128)(2,1)S(1)} %get-tuple-element.179, f32[8,512]{1,0:T(8,128)S(1)} %broadcast_divide_fusion.2, f32[4,8,3,512]{3,1,0,2:T(8,128)S(1)} %get-tuple-element.153, ...), kind=kOutput, calls=%fused_computation.5.clone.1 | convolution fusion | flops 212336640 | bytes 3817984 | tf_op jit(solution)/shard_map/while/body/eval_jaxpr/ikedp,jdep->ijk/dot_general | solution.py:81
  67.7 1.0 fusion.18
  69.1 2.2 %fusion.19 = f32[16,32,64,4]{2,1,3,0:T(8,128)} fusion(f32[16,32,64,4]{2,1,3,0:T(8,128)} %get-tuple-element.168, s32[]{:T(128)} %get-tuple-element.167, bf16[64,3,8,512]{3,0,2,1:T(8,128)(2,1)S(1)} %get-tuple-element.179, f32[8,512]{1,0:T(8,128)S(1)} %broadcast_divide_fusion.2, f32[4,8,3,512]{3,1,0,2:T(8,128)S(1)} %get-tuple-element.153, ...), kind=kOutput, calls=%fused_computation.5.clone.1 | convolution fusion | flops 212336640 | bytes 3817984 | tf_op jit(solution)/shard_map/while/body/eval_jaxpr/ikedp,jdep->ijk/dot_general | solution.py:81
  71.2 1.0 fusion.18
  72.6 2.1 %fusion.19 = f32[16,32,64,4]{2,1,3,0:T(8,128)} fusion(f32[16,32,64,4]{2,1,3,0:T(8,128)} %get-tuple-element.168, s32[]{:T(128)} %get-tuple-element.167, bf16[64,3,8,512]{3,0,2,1:T(8,128)(2,1)S(1)} %get-tuple-element.179, f32[8,512]{1,0:T(8,128)S(1)} %broadcast_divide_fusion.2, f32[4,8,3,512]{3,1,0,2:T(8,128)S(1)} %get-tuple-element.153, ...), kind=kOutput, calls=%fused_computation.5.clone.1 | convolution fusion | flops 212336640 | bytes 3817984 | tf_op jit(solution)/shard_map/while/body/eval_jaxpr/ikedp,jdep->ijk/dot_general | solution.py:81
  74.7 1.0 fusion.18
  76.1 2.2 %fusion.19 = f32[16,32,64,4]{2,1,3,0:T(8,128)} fusion(f32[16,32,64,4]{2,1,3,0:T(8,128)} %get-tuple-element.168, s32[]{:T(128)} %get-tuple-element.167, bf16[64,3,8,512]{3,0,2,1:T(8,128)(2,1)S(1)} %get-tuple-element.179, f32[8,512]{1,0:T(8,128)S(1)} %broadcast_divide_fusion.2, f32[4,8,3,512]{3,1,0,2:T(8,128)S(1)} %get-tuple-element.153, ...), kind=kOutput, calls=%fused_computation.5.clone.1 | convolution fusion | flops 212336640 | bytes 3817984 | tf_op jit(solution)/shard_map/while/body/eval_jaxpr/ikedp,jdep->ijk/dot_general | solution.py:81
  78.2 1.0 fusion.18
  79.6 2.2 %fusion.19 = f32[16,32,64,4]{2,1,3,0:T(8,128)} fusion(f32[16,32,64,4]{2,1,3,0:T(8,128)} %get-tuple-element.168, s32[]{:T(128)} %get-tuple-element.167, bf16[64,3,8,512]{3,0,2,1:T(8,128)(2,1)S(1)} %get-tuple-element.179, f32[8,512]{1,0:T(8,128)S(1)} %broadcast_divide_fusion.2, f32[4,8,3,512]{3,1,0,2:T(8,128)S(1)} %get-tuple-element.153, ...), kind=kOutput, calls=%fused_computation.5.clone.1 | convolution fusion | flops 212336640 | bytes 3817984 | tf_op jit(solution)/shard_map/while/body/eval_jaxpr/ikedp,jdep->ijk/dot_general | solution.py:81
  81.7 1.0 fusion.18
  83.1 2.2 %fusion.19 = f32[16,32,64,4]{2,1,3,0:T(8,128)} fusion(f32[16,32,64,4]{2,1,3,0:T(8,128)} %get-tuple-element.168, s32[]{:T(128)} %get-tuple-element.167, bf16[64,3,8,512]{3,0,2,1:T(8,128)(2,1)S(1)} %get-tuple-element.179, f32[8,512]{1,0:T(8,128)S(1)} %broadcast_divide_fusion.2, f32[4,8,3,512]{3,1,0,2:T(8,128)S(1)} %get-tuple-element.153, ...), kind=kOutput, calls=%fused_computation.5.clone.1 | convolution fusion | flops 212336640 | bytes 3817984 | tf_op jit(solution)/shard_map/while/body/eval_jaxpr/ikedp,jdep->ijk/dot_general | solution.py:81
  85.2 1.0 fusion.18
  86.6 2.2 %fusion.19 = f32[16,32,64,4]{2,1,3,0:T(8,128)} fusion(f32[16,32,64,4]{2,1,3,0:T(8,128)} %get-tuple-element.168, s32[]{:T(128)} %get-tuple-element.167, bf16[64,3,8,512]{3,0,2,1:T(8,128)(2,1)S(1)} %get-tuple-element.179, f32[8,512]{1,0:T(8,128)S(1)} %broadcast_divide_fusion.2, f32[4,8,3,512]{3,1,0,2:T(8,128)S(1)} %get-tuple-element.153, ...), kind=kOutput, calls=%fused_computation.5.clone.1 | convolution fusion | flops 212336640 | bytes 3817984 | tf_op jit(solution)/shard_map/while/body/eval_jaxpr/ikedp,jdep->ijk/dot_general | solution.py:81
  88.7 1.0 fusion.18
  90.1 2.1 %fusion.19 = f32[16,32,64,4]{2,1,3,0:T(8,128)} fusion(f32[16,32,64,4]{2,1,3,0:T(8,128)} %get-tuple-element.168, s32[]{:T(128)} %get-tuple-element.167, bf16[64,3,8,512]{3,0,2,1:T(8,128)(2,1)S(1)} %get-tuple-element.179, f32[8,512]{1,0:T(8,128)S(1)} %broadcast_divide_fusion.2, f32[4,8,3,512]{3,1,0,2:T(8,128)S(1)} %get-tuple-element.153, ...), kind=kOutput, calls=%fused_computation.5.clone.1 | convolution fusion | flops 212336640 | bytes 3817984 | tf_op jit(solution)/shard_map/while/body/eval_jaxpr/ikedp,jdep->ijk/dot_general | solution.py:81
  92.2 1.0 fusion.18
  93.3 0.2 slice_bitcast_fusion.9
  93.6 2.2 %fusion.19 = f32[16,32,64,4]{2,1,3,0:T(8,128)} fusion(f32[16,32,64,4]{2,1,3,0:T(8,128)} %get-tuple-element.168, s32[]{:T(128)} %get-tuple-element.167, bf16[64,3,8,512]{3,0,2,1:T(8,128)(2,1)S(1)} %get-tuple-element.179, f32[8,512]{1,0:T(8,128)S(1)} %broadcast_divide_fusion.2, f32[4,8,3,512]{3,1,0,2:T(8,128)S(1)} %get-tuple-element.153, ...), kind=kOutput, calls=%fused_computation.5.clone.1 | convolution fusion | flops 212336640 | bytes 3817984 | tf_op jit(solution)/shard_map/while/body/eval_jaxpr/ikedp,jdep->ijk/dot_general | solution.py:81
  95.7 3.1 %copy.29 = f32[32,64,64]{2,0,1:T(8,128)} copy(f32[32,64,64]{1,0,2:T(8,128)} %bitcast.6) | data formatting | bytes 1048576 | tf_op jit(solution)/shard_map/reshape | solution.py:86
  98.9 58.3 %reduce-scatter.2.cloned.1.call-done = f32[32,4,64]{2,0,1:T(8,128)} async-done(((f32[32,64,64]{2,0,1:T(8,128)}), f32[32,4,64]{2,0,1:T(8,128)}) %reduce-scatter.2.cloned.1.call-update) | async-done | bytes 32784 | tf_op jit(solution)/shard_map/reduce_scatter | solution.py:106
  157.2 0.8 broadcast_multiply_fusion
  158.0 0.7 copy.30
  (63 shorter events, 4.8 us)
Async XLA Ops:
  6.5 7.2 %copy-start = (bf16[32,3,4096]{2,0,1:T(8,128)(2,1)S(1)}, bf16[32,3,4096]{2,0,1:T(8,128)(2,1)}, u32[]{:S(2)}) copy-start(bf16[32,3,4096]{2,0,1:T(8,128)(2,1)} %param.7) | copy-start | bytes 2359300
  9.3 5.7 %copy-start.2 = (f32[4,3]{1,0:T(4,128)S(1)}, f32[4,3]{1,0:T(4,128)}, u32[]{:S(2)}) copy-start(f32[4,3]{1,0:T(4,128)} %param.9) | copy-start | bytes 148
  9.3 24.5 %all-to-all-start = ((bf16[2,32,3,4096]{3,1,2,0:T(8,128)(2,1)}), bf16[2,32,3,4096]{3,1,2,0:T(8,128)(2,1)S(1)}, u32[]{:S(2)}, u32[]{:S(2)}) async-start(bf16[2,32,3,4096]{3,1,2,0:T(8,128)(2,1)} %pad_maximum_fusion), calls=%async_computation | async-start | bytes 3145728 | tf_op jit(solution)/shard_map/all_to_all | solution.py:10
  13.7 3.0 %copy-start.3 = (s32[8]{0:T(128)S(1)}, s32[8]{0:T(128)}, u32[]{:S(2)}) copy-start(s32[8]{0:T(128)} %param.8) | copy-start | bytes 100
  13.7 143.5 %reduce-scatter.2.cloned.1.call-start = ((), (), s32[]{:S(2)}) async-start(), calls=%async_computation.2 | async-start | bytes 1114112 | tf_op jit(solution)/shard_map/reduce_scatter | solution.py:106
  34.0 1.4 copy-start.4
  35.4 4.3 %copy-start.1 = (f32[512]{0:T(512)S(1)}, f32[512]{0:T(512)}, u32[]{:S(2)}) copy-start(f32[512]{0:T(512)} %constant.23.clone) | copy-start | bytes 6148
Sparse Core Ops, SparseCore 0:
  99.0 58.1 reduce-scatter.1
